TPU v7x, 32 devices: a whole 2x2x4 slice. The times are simulated.
32 devices in a mesh: groups: 2 (over y), ep: 4 (over x, core), tp: 4 (over z).
Axes of the slice: x: 2, y: 2, z: 4, core: 2. Of those that a mesh axis runs over, the one named last changes fastest.
Arguments:
- tokens: bfloat16 [256, 7168], P(('groups', 'ep')), parts along dimension 0, may hold values from -6 to 6
- w_gate: bfloat16 [16, 7168, 2048], P('ep', None, 'tp'), may hold values from -0.0625 to 0.0625
- w_up: bfloat16 [16, 7168, 2048], P('ep', None, 'tp'), may hold values from -0.0625 to 0.0625
- w_down: bfloat16 [16, 2048, 7168], P('ep', 'tp'), may hold values from -0.1875 to 0.1875
- router_logits: float32 [256, 8], P(('groups', 'ep')), parts along dimension 0, may hold values from -6 to 6
- expert_ids: int32 [256, 8], P(('groups', 'ep')), parts along dimension 0, may hold values from 0 to 15, all different within a row; in each aligned block of 32 rows (0 to 31, 32 to 63, ...) at most 24 rows name the same one
- draft_lengths: int32 [32], P(('groups', 'ep')), parts along dimension 0, may hold values from 7 to 8
- accept_mask: int32 [32, 8], P(('groups', 'ep')), parts along dimension 0, may hold values 0 or 1
Outputs:
- mixed: bfloat16 [256, 7168], P(('groups', 'ep'), 'tp'), parts along dimension 0
- accepted: int32 [2], P('groups'), parts along dimension 0
There are 2 independent parts, one for each index of `groups`. A program takes and returns all parts, laid end to end along the dimension named above; an argument that names none is the same for every part. Nothing has to cross between parts.
Inputs may be any that keep to these rules, and one draw needn't show every extreme that they name: `expert_ids`: each row names 8 different experts. Among the rows of one ep index (aligned blocks of 32 rows) no expert is named by more than 24 rows, and in every draw some expert is named by exactly 24 rows of some block.
All inputs are finite; a program needn't handle non-finite values. No bound on the sum of `accept_mask` on one device may be relied on, other than what follows from the above.
Results may differ from a plain program's by a relative error of at most 0.017.
Values may be sent and summed in bfloat16 or wider, within the bound.
A program may use at most 192 MiB of HBM per device.

v0:
```python
import jax
import jax.numpy as jnp
from jax import lax
from jax.sharding import PartitionSpec as P

DRAFT = 8
EXPERTS = 16


def per_device(tokens, w_gate, w_up, w_down, router_logits, expert_ids, draft_lengths, accept_mask):
    tok_rows = tokens.shape[0]
    local = w_gate.shape[0]
    me = lax.axis_index("ep")
    live = jnp.arange(DRAFT, dtype=jnp.int32)[None, :] < draft_lengths[:, None]
    sig = jax.nn.sigmoid(router_logits)
    gates = 2.827 * sig / jnp.sum(sig, axis=1, keepdims=True)
    named = expert_ids[:, :, None] == jnp.arange(EXPERTS, dtype=jnp.int32)[None, None, :]
    dense = jnp.sum(jnp.where(named, gates[:, :, None], 0.0), axis=1)
    dense = jnp.where(live.reshape(tok_rows)[:, None], dense, 0.0)
    rows = lax.all_gather(tokens, "ep", axis=0, tiled=True)
    dense = lax.all_gather(dense, "ep", axis=0, tiled=True)
    mine = lax.dynamic_slice_in_dim(dense, me * local, local, axis=1)
    gate = jnp.einsum("md,edf->emf", rows, w_gate, preferred_element_type=jnp.float32)
    up = jnp.einsum("md,edf->emf", rows, w_up, preferred_element_type=jnp.float32)
    hidden = (jax.nn.silu(gate) * up * mine.T[:, :, None]).astype(jnp.bfloat16)
    partial = jnp.einsum("emf,efd->md", hidden, w_down, preferred_element_type=jnp.float32)
    partial = partial.astype(jnp.bfloat16)
    partial = lax.psum_scatter(partial, "ep", scatter_dimension=0, tiled=True)
    mixed = lax.psum_scatter(partial, "tp", scatter_dimension=1, tiled=True)
    passed = accept_mask * live.astype(jnp.int32)
    accepted = lax.psum(jnp.sum(jnp.cumprod(passed, axis=1)), "ep").reshape(1)
    return (mixed, accepted)


def solution(mesh):
    placed = (
        P(("groups", "ep"), None),
        P("ep", None, "tp"),
        P("ep", None, "tp"),
        P("ep", "tp", None),
        P(("groups", "ep"), None),
        P(("groups", "ep"), None),
        P(("groups", "ep")),
        P(("groups", "ep"), None),
    )
    return jax.shard_map(
        per_device,
        mesh=mesh,
        in_specs=placed,
        out_specs=(P(("groups", "ep"), "tp"), P("groups")),
        check_vma=False,
    )
```

profile of v0, /device:TPU:0, one launch (start us, length us, event | category | flops | bytes accessed | tf_op | source)
XLA Modules:
  0.0 140.5 jit_solution(3762252298330406964)
XLA Ops:
  7.2 0.0 all-gather.3.cloned.1.call-start
  7.2 0.7 all-gather.3.cloned.1.call-update
  7.9 0.0 reduce-scatter.3.cloned.1.call-start
  7.9 0.7 iota_compare_fusion.1
  8.7 0.1 lt.26
  8.8 0.7 fusion.20
  9.5 0.7 multiply_divide_fusion
  10.2 0.7 select_reduce_fusion
  10.9 6.2 %all-gather = f32[4,32,16]{1,2,0:T(8,128)S(1)} all-gather(f32[1,32,16]{1,2,0:T(8,128)S(1)} %select_bitcast_fusion), channel_id=1, replica_groups=mesh['groups'=2,'ep'=4,'tp'=4] {'ep'}, dimensions={0}, use_global_device_ids=true | all-gather | bytes 10240 | tf_op jit(solution)/shard_map/all_gather | solution.py:21
  17.1 0.1 reshape.28
  17.2 16.2 %all-gather.3.cloned.1.call-done = bf16[128,7168]{1,0:T(8,128)(2,1)} async-done(((bf16[32,7168]{1,0:T(8,128)(2,1)}), bf16[128,7168]{1,0:T(8,128)(2,1)}) %all-gather.3.cloned.1.call-update) | async-done | bytes 1835024 | tf_op jit(solution)/shard_map/all_gather | solution.py:20
  33.4 0.0 copy-start.2
  33.4 17.8 %fusion.5 = f32[4,128,512]{1,2,0:T(8,128)S(1)} fusion(bf16[4,7168,512]{2,1,0:T(8,128)(2,1)} %param.9, bf16[128,7168]{1,0:T(8,128)(2,1)} %all-gather.3.cloned.1.call-done), kind=kOutput, calls=%fused_computation.6 | convolution fusion | flops 3758096384 | bytes 32243712 | tf_op jit(solution)/shard_map/md,edf->emf/dot_general | solution.py:23
  51.2 0.0 copy-done.2
  51.2 0.0 copy-start
  51.2 0.0 copy-start.1
  51.2 14.0 %fusion.17 = bf16[4,128,512]{1,2,0:T(8,128)(2,1)S(1)} fusion(bf16[4,7168,512]{2,1,0:T(8,128)(2,1)} %param.10, bf16[128,7168]{1,0:T(8,128)(2,1)S(1)} %copy-done.2, f32[4,128,512]{1,2,0:T(8,128)S(1)} %fusion.5, f32[4,128]{1,0:T(4,128)S(1)} %dynamic-slice_bitcast_fusion), kind=kOutput, calls=%fused_computation.10 | convolution fusion | flops 3759931392 | bytes 32770048 | tf_op jit(solution)/shard_map/md,edf->emf/dot_general | solution.py:24
  65.2 14.8 %fusion = bf16[128,7168]{1,0:T(8,128)(2,1)} fusion(bf16[4,128,512]{1,2,0:T(8,128)(2,1)S(1)} %fusion.17, bf16[4,512,7168]{2,1,0:T(8,128)(2,1)} %param.11), kind=kOutput, calls=%fused_computation.1 | convolution fusion | flops 3759013888 | bytes 31719424 | tf_op jit(solution)/shard_map/emf,efd->md/dot_general | solution.py:26
  80.0 0.0 reduce-scatter.3.cloned.1.call-update
  80.0 0.0 reduce-scatter.5.cloned.1.call-start
  80.1 29.7 %reduce-scatter.3.cloned.1.call-done = bf16[32,7168]{1,0:T(8,128)(2,1)} async-done(((bf16[128,7168]{1,0:T(8,128)(2,1)}), bf16[32,7168]{1,0:T(8,128)(2,1)}) %reduce-scatter.3.cloned.1.call-update) | async-done | bytes 458768 | tf_op jit(solution)/shard_map/reduce_scatter | solution.py:28
  109.8 0.0 reduce-scatter.5.cloned.1.call-update
  109.8 0.0 copy-done
  109.8 0.0 copy-done.1
  109.8 0.1 broadcast_select_fusion
  109.9 0.2 reduce_window.9
  110.1 0.6 reduce_sum.29
  110.7 4.9 %psum.7 = s32[1]{0:T(128)} all-reduce(s32[1]{0:T(128)} %bitcast.6), channel_id=1, replica_groups=mesh['groups'=2,'ep'=4,'tp'=4] {'ep'}, use_global_device_ids=true, to_apply=%region_6.7 | all-reduce | flops 1 | bytes 8 | tf_op jit(solution)/shard_map/psum | solution.py:31
  115.6 18.4 %reduce-scatter.5.cloned.1.call-done = bf16[32,1792]{1,0:T(8,128)(2,1)} async-done(((bf16[32,7168]{1,0:T(8,128)(2,1)}), bf16[32,1792]{1,0:T(8,128)(2,1)}) %reduce-scatter.5.cloned.1.call-update) | async-done | bytes 114704 | tf_op jit(solution)/shard_map/reduce_scatter | solution.py:29
  (3 shorter events, 0.0 us)
Async XLA Ops:
  7.2 26.2 %all-gather.3.cloned.1.call-start = ((), (), s32[]{:S(2)}) async-start(), calls=%async_computation.2 | async-start | bytes 2293760 | tf_op jit(solution)/shard_map/all_gather | solution.py:20
  7.9 101.9 %reduce-scatter.3.cloned.1.call-start = ((), (), s32[]{:S(2)}) async-start(), calls=%async_computation.3 | async-start | bytes 2293760 | tf_op jit(solution)/shard_map/reduce_scatter | solution.py:28
  33.4 17.8 %copy-start.2 = (bf16[128,7168]{1,0:T(8,128)(2,1)S(1)}, bf16[128,7168]{1,0:T(8,128)(2,1)}, u32[]{:S(2)}) copy-start(bf16[128,7168]{1,0:T(8,128)(2,1)} %all-gather.3.cloned.1.call-done) | copy-start | bytes 5505028
  51.2 58.6 %copy-start = (s32[4,8]{1,0:T(4,128)S(1)}, s32[4,8]{1,0:T(4,128)}, u32[]{:S(2)}) copy-start(s32[4,8]{1,0:T(4,128)} %param.15) | copy-start | bytes 388
  51.2 58.6 %copy-start.1 = (s32[4]{0:T(128)S(1)}, s32[4]{0:T(128)}, u32[]{:S(2)}) copy-start(s32[4]{0:T(128)} %param.14) | copy-start | bytes 52
  80.0 54.0 %reduce-scatter.5.cloned.1.call-start = ((), (), s32[]{:S(2)}) async-start(), calls=%async_computation.4 | async-start | bytes 573440 | tf_op jit(solution)/shard_map/reduce_scatter | solution.py:29
Sparse Core Ops, SparseCore 0:
  9.5 23.8 all-gather.2
  80.2 29.5 reduce-scatter.2
  112.6 21.3 reduce-scatter.4
where the time goes:
time: 141 us
  waiting for transfers between devices  65 us (46%)
  matrix products  46.6 us (33%)
  between operations  13.8 us (10%)
  blocking collectives  11.1 us (8%)
  other arithmetic  3.75 us (3%)
    reduce_scatter x1, waiting for transfers between devices, per_device(): partial = lax.psum_scatter(partial, 'ep', scatter_dimension=0, tiled=True)  29.7 us
    reduce_scatter x1, waiting for transfers between devices, per_device(): mixed = lax.psum_scatter(partial, 'tp', scatter_dimension=1, tiled=True)  18.4 us
    dot_general x1, matrix products, per_device(): jnp.einsum('md,edf->emf', rows, w_gate, preferred_element_type=jnp.float32)  17.8 us
    all_gather x1, waiting for transfers between devices, per_device(): rows = lax.all_gather(tokens, 'ep', axis=0, tiled=True)  16.2 us
    dot_general x1, matrix products, per_device(): jnp.einsum('emf,efd->md', hidden, w_down, preferred_element_type=jnp.floa...  14.8 us
    dot_general x1, matrix products, per_device(): jnp.einsum('md,edf->emf', rows, w_up, preferred_element_type=jnp.float32)  14 us
    all_gather x1, blocking collectives, per_device(): dense = lax.all_gather(dense, 'ep', axis=0, tiled=True)  6.21 us
    psum x1, blocking collectives, per_device(): accepted = lax.psum(jnp.sum(jnp.cumprod(passed, axis=1)), 'ep').reshape(1)  4.89 us
  transfers between devices with their start and end apart: 3, of which 3 were waited for; matrix products, arithmetic and copies ran while one was open for 3% of the time, Pallas kernels for 0%

commit v1 on v0

--- a/solution.py
+++ b/solution.py
@@ -1,3 +1,4 @@
+import functools
 import jax
 import jax.numpy as jnp
 from jax import lax
@@ -5,6 +6,26 @@
 
 DRAFT = 8
 EXPERTS = 16
+
+
+def resolve_record(my_tile, pos_dim):
+    extent = lax.axis_size("ep")
+    val = range(1, extent)
+    odd = map(lambda nth: (nth - 1, nth), val)
+    main = list(odd)
+    left_arr = my_tile
+    carry = main + [(extent - 1, 0)]
+    by_rank = [left_arr]
+    for _ in range(extent - 1):
+        left_arr = lax.ppermute(left_arr, axis_name="ep", perm=carry)
+        by_rank += [left_arr]
+    carry_out = jnp.concatenate([*reversed(by_rank)], pos_dim)
+    after = lax.axis_index("ep")
+    later = jnp.roll(carry_out, (after + 1) * left_arr.shape[pos_dim], pos_dim)
+    return later
+
+
+vectors_expand = functools.partial(resolve_record, pos_dim=0)
 
 
 def per_device(tokens, w_gate, w_up, w_down, router_logits, expert_ids, draft_lengths, accept_mask):
@@ -17,7 +38,7 @@
     named = expert_ids[:, :, None] == jnp.arange(EXPERTS, dtype=jnp.int32)[None, None, :]
     dense = jnp.sum(jnp.where(named, gates[:, :, None], 0.0), axis=1)
     dense = jnp.where(live.reshape(tok_rows)[:, None], dense, 0.0)
-    rows = lax.all_gather(tokens, "ep", axis=0, tiled=True)
+    rows = vectors_expand(tokens)
     dense = lax.all_gather(dense, "ep", axis=0, tiled=True)
     mine = lax.dynamic_slice_in_dim(dense, me * local, local, axis=1)
     gate = jnp.einsum("md,edf->emf", rows, w_gate, preferred_element_type=jnp.float32)

time: 141 us -> 133 us (0.943)
  matrix products: 46.6 us -> 33.6 us
  local copies, waits for them, and re-layouts: 0.21 us -> 3.27 us
    all_gather x1 -> x0, waiting for transfers between devices: 16.2 us -> none  [per_device(): rows = lax.all_gather(tokens, 'ep', axis=0, tiled=True)]
    ppermute x0 -> x3, waiting for transfers between devices: none -> 14.7 us  [resolve_record(): left_arr = lax.ppermute(left_arr, axis_name='ep', perm=carry)]
    dot_general x1 -> x0, matrix products: 14 us -> none  [per_device(): jnp.einsum('md,edf->emf', rows, w_up, preferred_element_type=jnp.float32)]
    dot_general x1, matrix products: 14.8 us -> 22.2 us  [per_device(): jnp.einsum('emf,efd->md', hidden, w_down, preferred_element_type=jnp.floa...]
    dot_general x1, matrix products: 17.8 us -> 11.4 us  [per_device(): jnp.einsum('md,edf->emf', rows, w_gate, preferred_element_type=jnp.float32)]
    unnamed x7 -> x16, local copies, waits for them, and re-layouts: 0.1 us -> 3.13 us
    reduce_scatter x1, waiting for transfers between devices: 29.7 us -> 31.7 us  [per_device(): partial = lax.psum_scatter(partial, 'ep', scatter_dimension=0, tiled=True)]
  transfers between devices with their start and end apart: 3 -> 5, of which waited for: 3 -> 4; matrix products, arithmetic and copies ran while one was open for 3% -> 3% of each run, Pallas kernels for 0% -> 0%
where the time goes in v1:
time: 133 us
  waiting for transfers between devices  64.9 us (49%)
  matrix products  33.6 us (25%)
  between operations  14.2 us (11%)
  blocking collectives  12.2 us (9%)
  other arithmetic  3.74 us (3%)
  local copies, waits for them, and re-layouts  3.27 us (2%)
    reduce_scatter x1, waiting for transfers between devices, per_device(): partial = lax.psum_scatter(partial, 'ep', scatter_dimension=0, tiled=True)  31.7 us
    dot_general x1, matrix products, per_device(): jnp.einsum('emf,efd->md', hidden, w_down, preferred_element_type=jnp.floa...  22.2 us
    reduce_scatter x1, waiting for transfers between devices, per_device(): mixed = lax.psum_scatter(partial, 'tp', scatter_dimension=1, tiled=True)  18.4 us
    ppermute x3, waiting for transfers between devices, resolve_record(): left_arr = lax.ppermute(left_arr, axis_name='ep', perm=carry)  14.7 us
    dot_general x1, matrix products, per_device(): jnp.einsum('md,edf->emf', rows, w_gate, preferred_element_type=jnp.float32)  11.4 us
    all_gather x1, blocking collectives, per_device(): dense = lax.all_gather(dense, 'ep', axis=0, tiled=True)  7.28 us
    psum x1, blocking collectives, per_device(): accepted = lax.psum(jnp.sum(jnp.cumprod(passed, axis=1)), 'ep').reshape(1)  4.89 us
    unnamed x16, local copies, waits for them, and re-layouts  3.13 us
  transfers between devices with their start and end apart: 5, of which 4 were waited for; matrix products, arithmetic and copies ran while one was open for 3% of the time, Pallas kernels for 0%

profile of v1, /device:TPU:0, one launch (start us, length us, event | category | flops | bytes accessed | tf_op | source)
XLA Modules:
  0.0 132.5 jit_solution(2306946564197831017)
XLA Ops:
  7.2 0.0 copy-start
  7.2 0.0 reduce-scatter.3.cloned.1.call-start
  7.2 0.5 collective-permute-start
  7.8 8.3 %collective-permute-done = bf16[32,7168]{1,0:T(8,128)(2,1)S(1)} collective-permute-done((bf16[32,7168]{1,0:T(8,128)(2,1)}, bf16[32,7168]{1,0:T(8,128)(2,1)S(1)}, u32[]{:S(2)}, u32[]{:S(2)}) %collective-permute-start) | collective-permute-done | bytes 458784 | tf_op jit(solution)/shard_map/ppermute | solution.py:20
  16.1 0.0 collective-permute-start.1
  16.1 0.7 fusion.15
  16.8 0.7 multiply_divide_fusion
  17.5 6.5 %collective-permute-done.1 = bf16[32,7168]{1,0:T(8,128)(2,1)S(1)} collective-permute-done((bf16[32,7168]{1,0:T(8,128)(2,1)S(1)}, bf16[32,7168]{1,0:T(8,128)(2,1)S(1)}, u32[]{:S(2)}, u32[]{:S(2)}) %collective-permute-start.1) | collective-permute-done | bytes 458784 | tf_op jit(solution)/shard_map/ppermute | solution.py:20
  24.0 0.0 collective-permute-start.2
  24.0 0.7 iota_compare_fusion.1
  24.7 0.1 lt.40
  24.8 0.7 select_reduce_fusion
  25.5 7.3 %all-gather = f32[4,32,16]{1,2,0:T(8,128)S(1)} all-gather(f32[1,32,16]{1,2,0:T(8,128)S(1)} %select_bitcast_fusion), channel_id=1, replica_groups=mesh['groups'=2,'ep'=4,'tp'=4] {'ep'}, dimensions={0}, use_global_device_ids=true | all-gather | bytes 10240 | tf_op jit(solution)/shard_map/all_gather | solution.py:42
  32.8 0.1 reshape.28
  32.9 0.0 collective-permute-done.2
  33.0 1.1 constant_dynamic-update-slice_fusion.4
  34.2 0.0 copy-done
  34.2 0.0 copy-start.1
  34.2 1.8 %copy-done.1 = bf16[256,7168]{1,0:T(8,128)(2,1)} copy-done((bf16[256,7168]{1,0:T(8,128)(2,1)}, bf16[256,7168]{1,0:T(8,128)(2,1)S(1)}, u32[]{:S(2)}) %copy-start.1) | copy-done | bytes 3670040
  36.0 11.4 %fusion.7 = f32[4,128,512]{2,1,0:T(8,128)S(1)} fusion(bf16[4,7168,512]{2,1,0:T(8,128)(2,1)} %param.9, bf16[256,7168]{1,0:T(8,128)(2,1)S(1)} %constant_dynamic-update-slice_fusion, s32[]{:T(128)S(6)} %select_n.25), kind=kOutput, calls=%fused_computation.8 | convolution fusion | flops 3758096384 | bytes 32243716 | tf_op jit(solution)/shard_map/md,edf->emf/dot_general | solution.py:44
  47.5 0.0 copy-start.2
  47.5 0.0 copy-start.3
  47.5 22.2 %fusion = bf16[128,7168]{1,0:T(8,128)(2,1)} fusion(bf16[4,512,7168]{2,1,0:T(8,128)(2,1)} %param.11, f32[4,128,512]{2,1,0:T(8,128)S(1)} %fusion.7, f32[4,128]{1,0:T(4,128)S(1)} %dynamic-slice_bitcast_fusion, bf16[4,7168,512]{2,1,0:T(8,128)(2,1)} %param.10, bf16[256,7168]{1,0:T(8,128)(2,1)} %copy-done.1, s32[]{:T(128)S(6)} %select_n.25), kind=kOutput, calls=%fused_computation.1 | convolution fusion | flops 7518945280 | bytes 63440900 | tf_op jit(solution)/shard_map/emf,efd->md/dot_general | solution.py:47
  69.7 0.0 reduce-scatter.3.cloned.1.call-update
  69.7 0.0 reduce-scatter.5.cloned.1.call-start
  69.7 31.7 %reduce-scatter.3.cloned.1.call-done = bf16[32,7168]{1,0:T(8,128)(2,1)} async-done(((bf16[128,7168]{1,0:T(8,128)(2,1)}), bf16[32,7168]{1,0:T(8,128)(2,1)}) %reduce-scatter.3.cloned.1.call-update) | async-done | bytes 458768 | tf_op jit(solution)/shard_map/reduce_scatter | solution.py:49
  101.5 0.0 reduce-scatter.5.cloned.1.call-update
  101.5 0.0 copy-done.2
  101.5 0.0 copy-done.3
  101.5 0.1 broadcast_select_fusion
  101.6 0.2 reduce_window.9
  101.8 0.6 reduce_sum.29
  102.4 4.9 %psum.7 = s32[1]{0:T(128)} all-reduce(s32[1]{0:T(128)} %bitcast.6), channel_id=1, replica_groups=mesh['groups'=2,'ep'=4,'tp'=4] {'ep'}, use_global_device_ids=true, to_apply=%region_6.7 | all-reduce | flops 1 | bytes 8 | tf_op jit(solution)/shard_map/psum | solution.py:52
  107.3 18.4 %reduce-scatter.5.cloned.1.call-done = bf16[32,1792]{1,0:T(8,128)(2,1)} async-done(((bf16[32,7168]{1,0:T(8,128)(2,1)}), bf16[32,1792]{1,0:T(8,128)(2,1)}) %reduce-scatter.5.cloned.1.call-update) | async-done | bytes 114704 | tf_op jit(solution)/shard_map/reduce_scatter | solution.py:50
  (10 shorter events, 0.3 us)
Async XLA Ops:
  7.2 27.0 %copy-start = (bf16[32,7168]{1,0:T(8,128)(2,1)S(1)}, bf16[32,7168]{1,0:T(8,128)(2,1)}, u32[]{:S(2)}) copy-start(bf16[32,7168]{1,0:T(8,128)(2,1)} %param.8) | copy-start | bytes 1376260
  7.2 94.3 %reduce-scatter.3.cloned.1.call-start = ((), (), s32[]{:S(2)}) async-start(), calls=%async_computation.2 | async-start | bytes 2293760 | tf_op jit(solution)/shard_map/reduce_scatter | solution.py:49
  7.2 8.8 %collective-permute-start = (bf16[32,7168]{1,0:T(8,128)(2,1)}, bf16[32,7168]{1,0:T(8,128)(2,1)S(1)}, u32[]{:S(2)}, u32[]{:S(2)}) collective-permute-start(bf16[32,7168]{1,0:T(8,128)(2,1)} %param.8), channel_id=1, source_target_pairs={{0,4},{4,8},{8,12},{12,0},{1,5},{5,9},{9,13},{13,1},{2,6},{6,10},{... | collective-permute-start | bytes 1376264 | tf_op jit(solution)/shard_map/ppermute | solution.py:20
  16.1 7.9 %collective-permute-start.1 = (bf16[32,7168]{1,0:T(8,128)(2,1)S(1)}, bf16[32,7168]{1,0:T(8,128)(2,1)S(1)}, u32[]{:S(2)}, u32[]{:S(2)}) collective-permute-start(bf16[32,7168]{1,0:T(8,128)(2,1)S(1)} %collective-permute-done), channel_id=1, source_target_pairs={{0,4},{4,8},{8,12},{12,0},{1,5},{5,9},{9,13},{13,1},{2,6},{6,10},{... | collective-permute-start | bytes 1376264 | tf_op jit(solution)/shard_map/ppermute | solution.py:20
  24.0 8.9 %collective-permute-start.2 = (bf16[32,7168]{1,0:T(8,128)(2,1)S(1)}, bf16[32,7168]{1,0:T(8,128)(2,1)S(1)}, u32[]{:S(2)}, u32[]{:S(2)}) collective-permute-start(bf16[32,7168]{1,0:T(8,128)(2,1)S(1)} %collective-permute-done.1), channel_id=1, source_target_pairs={{0,4},{4,8},{8,12},{12,0},{1,5},{5,9},{9,13},{13,1},{2,6},{6,10},{... | collective-permute-start | bytes 1376264 | tf_op jit(solution)/shard_map/ppermute | solution.py:20
  34.2 1.8 %copy-start.1 = (bf16[256,7168]{1,0:T(8,128)(2,1)}, bf16[256,7168]{1,0:T(8,128)(2,1)S(1)}, u32[]{:S(2)}) copy-start(bf16[256,7168]{1,0:T(8,128)(2,1)S(1)} %constant_dynamic-update-slice_fusion) | copy-start | bytes 11010052
  47.5 54.0 %copy-start.2 = (s32[4,8]{1,0:T(4,128)S(1)}, s32[4,8]{1,0:T(4,128)}, u32[]{:S(2)}) copy-start(s32[4,8]{1,0:T(4,128)} %param.15) | copy-start | bytes 388
  47.5 54.0 %copy-start.3 = (s32[4]{0:T(128)S(1)}, s32[4]{0:T(128)}, u32[]{:S(2)}) copy-start(s32[4]{0:T(128)} %param.14) | copy-start | bytes 52
  69.7 56.0 %reduce-scatter.5.cloned.1.call-start = ((), (), s32[]{:S(2)}) async-start(), calls=%async_computation.3 | async-start | bytes 573440 | tf_op jit(solution)/shard_map/reduce_scatter | solution.py:50
Sparse Core Ops, SparseCore 0:
  69.8 31.6 reduce-scatter.2
  104.3 21.2 reduce-scatter.4
